TPU v7x, 32 devices: a whole 2x2x4 slice. The times are simulated.
32 devices in a mesh: rows: 8 (over y, x, core), cols: 4 (over z).
Axes of the slice: x: 2, y: 2, z: 4, core: 2. Of those that a mesh axis runs over, the one named last changes fastest.
Arguments:
- w_query: bfloat16 [4096, 4096], P('rows', 'cols'), may hold values from -0.09375 to 0.09375
- low_query: bfloat16 [4096, 16], P('rows'), may hold values from -0.09375 to 0.09375
- high_query: bfloat16 [16, 4096], P(None, 'cols'), may hold values from -1.5 to 1.5
- w_key: bfloat16 [4096, 1024], P('rows', 'cols'), may hold values from -0.09375 to 0.09375
- low_key: bfloat16 [4096, 16], P('rows'), may hold values from -0.09375 to 0.09375
- high_key: bfloat16 [16, 1024], P(None, 'cols'), may hold values from -1.5 to 1.5
- w_value: bfloat16 [4096, 1024], P('rows', 'cols'), may hold values from -0.09375 to 0.09375
- low_value: bfloat16 [4096, 16], P('rows'), may hold values from -0.09375 to 0.09375
- high_value: bfloat16 [16, 1024], P(None, 'cols'), may hold values from -1.5 to 1.5
- w_mixed: bfloat16 [4096, 4096], P('cols', 'rows'), may hold values from -0.09375 to 0.09375
- low_mixed: bfloat16 [4096, 16], P('cols'), may hold values from -0.09375 to 0.09375
- high_mixed: bfloat16 [16, 4096], P(None, 'rows'), may hold values from -1.5 to 1.5
- norm_train: float32 [4096], P(('rows', 'cols')), may hold values from 0.25 to 1.75
- norm_step: float32 [4096], P(('rows', 'cols')), may hold values from -0.3 to 0.3
Outputs:
- serving_query: bfloat16 [4096, 4096], P(None, 'cols')
- serving_key: bfloat16 [4096, 1024], P(None, 'cols')
- serving_value: bfloat16 [4096, 1024], P(None, 'cols')
- serving_mixed: bfloat16 [4096, 4096], P('cols')
- serve_norm: bfloat16 [4096], replicated
All inputs are finite; a program needn't handle non-finite values.
Results may differ from a plain program's by a relative error of at most 0.001.
Values may be sent and summed in bfloat16 or wider, within the bound.
A program may use at most 128 MiB of HBM per device.

v0:
```python
import jax
import jax.numpy as jnp
from jax import lax
from jax.sharding import PartitionSpec as P

mix_rate = 1.0


def local(
    w_query,
    low_query,
    high_query,
    w_key,
    low_key,
    high_key,
    w_value,
    low_value,
    high_value,
    w_mixed,
    low_mixed,
    high_mixed,
    norm_train,
    norm_step,
):
    (
        moved_query,
        moved_key,
        moved_value,
        moved_mixed,
        factor_query,
        factor_key,
        factor_value,
        factor_mixed,
    ) = (
        lax.all_gather(w_query, "rows", axis=0, tiled=True),
        lax.all_gather(w_key, "rows", axis=0, tiled=True),
        lax.all_gather(w_value, "rows", axis=0, tiled=True),
        lax.all_gather(w_mixed, "rows", axis=1, tiled=True),
        lax.all_gather(low_query, "rows", axis=0, tiled=True),
        lax.all_gather(low_key, "rows", axis=0, tiled=True),
        lax.all_gather(low_value, "rows", axis=0, tiled=True),
        lax.all_gather(high_mixed, "rows", axis=1, tiled=True),
    )
    whole_query = moved_query.astype(jnp.float32) + mix_rate * jnp.dot(
        factor_query, high_query, preferred_element_type=jnp.float32
    )
    serving_query = whole_query.astype(jnp.bfloat16)
    whole_key = moved_key.astype(jnp.float32) + mix_rate * jnp.dot(
        factor_key, high_key, preferred_element_type=jnp.float32
    )
    serving_key = whole_key.astype(jnp.bfloat16)
    whole_value = moved_value.astype(jnp.float32) + mix_rate * jnp.dot(
        factor_value, high_value, preferred_element_type=jnp.float32
    )
    serving_value = whole_value.astype(jnp.bfloat16)
    whole_mixed = moved_mixed.astype(jnp.float32) + mix_rate * jnp.dot(
        low_mixed, factor_mixed, preferred_element_type=jnp.float32
    )
    serving_mixed = whole_mixed.astype(jnp.bfloat16)
    serve_norm = lax.all_gather(
        (norm_train + norm_step).astype(jnp.bfloat16), ("rows", "cols"), axis=0, tiled=True
    )
    return (serving_query, serving_key, serving_value, serving_mixed, serve_norm)


def solution(mesh):
    in_specs = (
        P("rows", "cols"),
        P("rows", None),
        P(None, "cols"),
        P("rows", "cols"),
        P("rows", None),
        P(None, "cols"),
        P("rows", "cols"),
        P("rows", None),
        P(None, "cols"),
        P("cols", "rows"),
        P("cols", None),
        P(None, "rows"),
        P(("rows", "cols")),
        P(("rows", "cols")),
    )
    out_specs = (P(None, "cols"), P(None, "cols"), P(None, "cols"), P("cols", None), P())
    return jax.shard_map(local, mesh=mesh, in_specs=in_specs, out_specs=out_specs, check_vma=False)
```

profile of v0, /device:TPU:0, one launch (start us, length us, event | category | flops | bytes accessed | tf_op | source)
XLA Modules:
  0.0 200.4 jit_solution(10462439958734486095)
XLA Ops:
  7.2 0.0 copy-start
  7.2 0.0 all-gather.8.cloned.1.call-start
  7.2 0.7 all-gather.8.cloned.1.call-update
  7.9 0.0 all-gather.10.cloned.1.call-start
  8.0 0.7 all-gather.10.cloned.1.call-update
  8.7 0.0 all-gather.12.cloned.1.call-start
  8.7 0.7 all-gather.12.cloned.1.call-update
  9.4 0.0 all-gather.6.cloned.1.call-start
  9.4 0.5 all-gather.6.cloned.1.call-update
  10.0 0.7 convert_bitcast_fusion
  10.7 70.0 %all-gather = bf16[32,1,128]{2,1,0:T(2,128)(2,1)S(1)} all-gather(bf16[1,1,128]{2,1,0:T(2,128)(2,1)S(1)} %convert_bitcast_fusion), channel_id=1, replica_groups=mesh['rows'=8,'cols'=4] {'rows','cols'}, dimensions={0}, use_global_device_ids=true | all-gather | bytes 8448 | tf_op jit(solution)/shard_map/all_gather | solution.py:60
  80.7 0.6 reduce
  81.3 8.8 %all_gather.34 = bf16[16,4096]{1,0:T(8,128)(2,1)S(1)} all-gather(bf16[16,512]{1,0:T(8,128)(2,1)} %param.25), channel_id=1, replica_groups=mesh['rows'=8,'cols'=4] {'rows'}, dimensions={1}, use_global_device_ids=true | all-gather | bytes 147456 | tf_op jit(solution)/shard_map/all_gather | solution.py:42
  90.1 9.0 %all_gather.28 = bf16[4096,16]{0,1:T(8,128)(2,1)S(1)} all-gather(bf16[512,16]{0,1:T(8,128)(2,1)} %param.15), channel_id=1, replica_groups=mesh['rows'=8,'cols'=4] {'rows'}, dimensions={0}, use_global_device_ids=true | all-gather | bytes 147456 | tf_op jit(solution)/shard_map/all_gather | solution.py:39
  99.1 8.8 %all_gather.30 = bf16[4096,16]{0,1:T(8,128)(2,1)S(1)} all-gather(bf16[512,16]{0,1:T(8,128)(2,1)} %param.18), channel_id=1, replica_groups=mesh['rows'=8,'cols'=4] {'rows'}, dimensions={0}, use_global_device_ids=true | all-gather | bytes 147456 | tf_op jit(solution)/shard_map/all_gather | solution.py:40
  108.0 9.4 %all_gather.32 = bf16[4096,16]{0,1:T(8,128)(2,1)S(1)} all-gather(bf16[512,16]{0,1:T(8,128)(2,1)} %param.21), channel_id=1, replica_groups=mesh['rows'=8,'cols'=4] {'rows'}, dimensions={0}, use_global_device_ids=true | all-gather | bytes 147456 | tf_op jit(solution)/shard_map/all_gather | solution.py:41
  117.4 0.0 all-gather.8.cloned.1.call-done
  117.4 3.7 %fusion = bf16[4096,256]{1,0:T(8,128)(2,1)} fusion(bf16[4096,16]{0,1:T(8,128)(2,1)S(1)} %all_gather.30, bf16[16,256]{1,0:T(8,128)(2,1)} %param.19, bf16[4096,256]{1,0:T(8,128)(2,1)} %all-gather.8.cloned.1.call-done), kind=kOutput, calls=%fused_computation.4 | convolution fusion | flops 36700160 | bytes 4333568 | tf_op jit(solution)/shard_map/dot_general | solution.py:48
  121.1 0.0 all-gather.10.cloned.1.call-done
  121.1 3.7 %fusion.1 = bf16[4096,256]{1,0:T(8,128)(2,1)} fusion(bf16[4096,16]{0,1:T(8,128)(2,1)S(1)} %all_gather.32, bf16[16,256]{1,0:T(8,128)(2,1)} %param.22, bf16[4096,256]{1,0:T(8,128)(2,1)} %all-gather.10.cloned.1.call-done), kind=kOutput, calls=%fused_computation.5 | convolution fusion | flops 36700160 | bytes 4333568 | tf_op jit(solution)/shard_map/dot_general | solution.py:52
  124.7 0.0 copy-start.1
  124.7 4.7 %all-gather.12.cloned.1.call-done = bf16[1024,4096]{1,0:T(8,128)(2,1)} async-done(((bf16[1024,512]{1,0:T(8,128)(2,1)}), bf16[1024,4096]{1,0:T(8,128)(2,1)}) %all-gather.12.cloned.1.call-update) | async-done | bytes 8388624 | tf_op jit(solution)/shard_map/all_gather | solution.py:38
  129.4 0.0 copy-done
  129.4 9.2 %add_convert_fusion = bf16[1024,4096]{1,0:T(8,128)(2,1)} fusion(bf16[1024,4096]{1,0:T(8,128)(2,1)} %all-gather.12.cloned.1.call-done, bf16[1024,16]{0,1:T(8,128)(2,1)S(1)} %copy-done, bf16[16,4096]{1,0:T(8,128)(2,1)S(1)} %all_gather.34), kind=kOutput, calls=%fused_computation | convolution fusion | flops 146800640 | bytes 16941056 | tf_op jit(solution)/shard_map/dot_general | solution.py:56
  138.6 46.1 %all-gather.6.cloned.1.call-done = bf16[4096,1024]{1,0:T(8,128)(2,1)} async-done(((bf16[512,1024]{1,0:T(8,128)(2,1)}), bf16[4096,1024]{1,0:T(8,128)(2,1)}) %all-gather.6.cloned.1.call-update) | async-done | bytes 8388624 | tf_op jit(solution)/shard_map/all_gather | solution.py:35
  184.7 0.0 copy-done.1
  184.7 9.1 %add_convert_fusion.1 = bf16[4096,1024]{1,0:T(8,128)(2,1)} fusion(bf16[4096,1024]{1,0:T(8,128)(2,1)} %all-gather.6.cloned.1.call-done, bf16[4096,16]{0,1:T(8,128)(2,1)S(1)} %all_gather.28, bf16[16,1024]{1,0:T(8,128)(2,1)S(1)} %copy-done.1), kind=kOutput, calls=%fused_computation.1 | convolution fusion | flops 146800640 | bytes 16941056 | tf_op jit(solution)/shard_map/dot_general | solution.py:44
Async XLA Ops:
  7.2 122.3 %copy-start = (bf16[1024,16]{0,1:T(8,128)(2,1)S(1)}, bf16[1024,16]{0,1:T(8,128)(2,1)}, u32[]{:S(2)}) copy-start(bf16[1024,16]{0,1:T(8,128)(2,1)} %param.24) | copy-start | bytes 98308
  7.2 110.2 %all-gather.8.cloned.1.call-start = ((), (), s32[]{:S(2)}) async-start(), calls=%async_computation.1 | async-start | bytes 2359296 | tf_op jit(solution)/shard_map/all_gather | solution.py:36
  7.9 113.1 %all-gather.10.cloned.1.call-start = ((), (), s32[]{:S(2)}) async-start(), calls=%async_computation.2 | async-start | bytes 2359296 | tf_op jit(solution)/shard_map/all_gather | solution.py:37
  8.7 120.8 %all-gather.12.cloned.1.call-start = ((), (), s32[]{:S(2)}) async-start(), calls=%async_computation.3 | async-start | bytes 9437184 | tf_op jit(solution)/shard_map/all_gather | solution.py:38
  9.4 175.3 %all-gather.6.cloned.1.call-start = ((), (), s32[]{:S(2)}) async-start(), calls=%async_computation | async-start | bytes 9437184 | tf_op jit(solution)/shard_map/all_gather | solution.py:35
  124.7 59.9 %copy-start.1 = (bf16[16,1024]{1,0:T(8,128)(2,1)S(1)}, bf16[16,1024]{1,0:T(8,128)(2,1)}, u32[]{:S(2)}) copy-start(bf16[16,1024]{1,0:T(8,128)(2,1)} %param.16) | copy-start | bytes 98308
Sparse Core Ops, SparseCore 0:
  9.9 30.3 all-gather.7
  42.2 27.5 all-gather.9
  71.7 57.7 all-gather.11
  131.2 53.4 all-gather.5
where the time goes:
time: 201 us; the launch traced here: 200 us
  blocking collectives  106 us (53%)
  waiting for transfers between devices  53.4 us (27%)
  matrix products  25.7 us (13%)
  between operations  13.8 us (7%)
    all_gather x1, blocking collectives, local(): lax.all_gather((norm_train + norm_step).astype(jnp.bfloat16), ('rows', 'c...  70 us
    all_gather x1, waiting for transfers between devices, local(): lax.all_gather(w_query, 'rows', axis=0, tiled=True)  46.1 us
    all_gather x1, blocking collectives, local(): lax.all_gather(low_value, 'rows', axis=0, tiled=True)  9.42 us
    dot_general x1, matrix products, local(): jnp.dot(low_mixed, factor_mixed, preferred_element_type=jnp.float32)  9.15 us
    dot_general x1, matrix products, local(): jnp.dot(factor_query, high_query, preferred_element_type=jnp.float32)  9.15 us
    all_gather x1, blocking collectives, local(): lax.all_gather(low_query, 'rows', axis=0, tiled=True)  9 us
    all_gather x1, blocking collectives, local(): lax.all_gather(low_key, 'rows', axis=0, tiled=True)  8.82 us
    all_gather x1, blocking collectives, local(): lax.all_gather(high_mixed, 'rows', axis=1, tiled=True)  8.82 us
  transfers between devices with their start and end apart: 4, of which 2 were waited for; matrix products, arithmetic and copies ran while one was open for 9% of the time, Pallas kernels for 0%

commit v1 on v0

v1 whole, which is shorter than its diff:
```python
import functools

import jax
import jax.numpy as jnp
from jax import lax
from jax.experimental import pallas as pl
from jax.experimental.pallas import tpu as pltpu
from jax.sharding import PartitionSpec as P

mix_rate = 1.0
SIDE = 2
LINK_CHUNK = 1 << 17


def merged(weight, low, high):
    return (
        weight.astype(jnp.float32)
        + mix_rate * jnp.dot(low, high, preferred_element_type=jnp.float32)
    ).astype(jnp.bfloat16)


def plan_chunks(shapes):
    chunks = []
    for index, (height, width) in enumerate(shapes):
        rows = max(16, min(height // 2, LINK_CHUNK // (2 * width)))
        chunks += [(index, first, rows) for first in range(0, height, rows)]
    return chunks


def kernel(
    cols,
    chunks,
    split_dims,
    *refs,
):
    weights, lows, highs = refs[0:4], refs[4:8], refs[8:12]
    norm_train, norm_step = refs[12:14]
    outs, norm_out = refs[14:18], refs[18]
    held = refs[19:23]
    norm_slots, norm_rows = refs[23:25]
    load_sem, send_sem, x_sem, y_sem, far_sem, mate_sem, norm_send, norm_recv = refs[25:]

    me, col = lax.axis_index("rows"), lax.axis_index("cols")
    core, x, y = me % 2, (me // 2) % 2, me // 4

    def row_of(yy, xx, cc):
        return (yy * SIDE + xx) * 2 + cc

    side = row_of(y, 1 - x, core)
    across = row_of(1 - y, x, core)
    far = row_of(1 - y, 1 - x, core)
    mate = row_of(y, x, 1 - core)

    def place(owner, chunk):
        index, first, rows = chunk
        if split_dims[index] == 0:
            height = weights[index].shape[0]
            return outs[index].at[pl.ds(pl.multiple_of(owner * height + first, 16), rows), :]
        width = weights[index].shape[1]
        return outs[index].at[
            pl.ds(first, rows), pl.ds(pl.multiple_of(owner * width, 128), width)
        ]

    def shards(index, count):
        if split_dims[index] == 0:
            return outs[index].at[pl.ds(0, count * weights[index].shape[0]), :]
        return outs[index].at[:, pl.ds(0, count * weights[index].shape[1])]

    def send(owner, number, target, recv):
        chunk = chunks[number]
        where = place(owner, chunk)
        pltpu.make_async_remote_copy(
            src_ref=where,
            dst_ref=where,
            send_sem=send_sem.at[chunk[0]],
            recv_sem=recv,
            device_id=(target, col),
            device_id_type=pl.DeviceIdType.MESH,
        ).start()

    def arrived(owner, number, recv):
        where = place(owner, chunks[number])
        pltpu.make_async_copy(where, where, recv).wait()

    def load(number):
        index, first, rows = chunks[number]
        piece = pl.ds(first, rows)
        return pltpu.make_async_copy(
            weights[index].at[piece, :], held[index].at[piece, :], load_sem.at[number]
        )

    for number in range(len(chunks)):
        load(number).start()

    barrier = pltpu.get_barrier_semaphore()
    partners = [(lax.rem(me + step, 8), col) for step in range(1, 8)]
    mates = [(me, lax.rem(col + step, cols)) for step in range(1, cols)]
    for partner in partners + mates:
        pl.semaphore_signal(
            barrier, inc=1, device_id=partner, device_id_type=pl.DeviceIdType.MESH
        )
    norm_slots[me, col] = norm_train[...] + norm_step[...]
    pl.semaphore_wait(barrier, len(partners) + len(mates))

    def send_own(number):
        index = chunks[number][0]
        send(me, number, side, x_sem.at[number])
        send(me, number, across, y_sem.at[number])
        send(me, number, mate, mate_sem.at[index])

    for number, (index, first, rows) in enumerate(chunks):
        load(number).wait()
        piece = pl.ds(first, rows)
        place(me, chunks[number])[...] = merged(
            held[index][piece, :],
            lows[index][piece, :],
            highs[index][...],
        )
        if number:
            send_own(number - 1)

    def norm_copy(block, target, way):
        return pltpu.make_async_remote_copy(
            src_ref=block,
            dst_ref=block,
            send_sem=norm_send.at[way],
            recv_sem=norm_recv.at[way],
            device_id=target,
            device_id_type=pl.DeviceIdType.MESH,
        )

    for partner in mates:
        norm_copy(norm_slots.at[me, col], partner, 0).start()
    send_own(len(chunks) - 1)

    for number in range(len(chunks)):
        index = chunks[number][0]
        arrived(side, number, x_sem.at[number])
        if number % 2 == 0:
            send(side, number, across, far_sem.at[number])
        send(side, number, mate, mate_sem.at[index])
        arrived(across, number, y_sem.at[number])
        if number % 2 == 1:
            send(across, number, side, far_sem.at[number])
        send(across, number, mate, mate_sem.at[index])
        if number == 2:
            some = norm_slots.at[0, pl.ds(0, cols - 1)]
            pltpu.make_async_copy(some, some, norm_recv.at[0]).wait()
            pltpu.make_async_copy(some, some, norm_send.at[0]).wait()
            for partner in partners:
                norm_copy(norm_slots.at[me], partner, 1).start()

    some = norm_slots.at[pl.ds(0, 7)]
    pltpu.make_async_copy(some, some, norm_recv.at[1]).wait()
    pltpu.make_async_copy(some, some, norm_send.at[1]).wait()
    for row in range(8):
        for at in range(cols):
            norm_rows[pl.ds(row * cols + at, 1), :] = norm_slots[row, at]
    norm_out[...] = norm_rows[...].astype(jnp.bfloat16)

    for number in range(len(chunks)):
        arrived(far, number, far_sem.at[number])
        send(far, number, mate, mate_sem.at[chunks[number][0]])

    for index in range(4):
        some = shards(index, 4)
        pltpu.make_async_copy(some, some, mate_sem.at[index]).wait()
        some = shards(index, 7)
        pltpu.make_async_copy(some, some, send_sem.at[index]).wait()


def gather_kernel(cols, weights, lows, highs, norm_train, norm_step):
    split_dims = (0, 0, 0, 1)
    shapes = [weight.shape for weight in weights]
    chunks = plan_chunks(shapes)
    full = [
        (height * 8, width) if dim == 0 else (height, width * 8)
        for (height, width), dim in zip(shapes, split_dims)
    ]
    rows, width = 8 * cols, norm_train.shape[0]
    whole = pl.BlockSpec(memory_space=pltpu.VMEM)
    count = len(chunks)
    results = pl.pallas_call(
        functools.partial(kernel, cols, chunks, split_dims),
        out_shape=[pltpu.VMEM(shape, jnp.bfloat16) for shape in full]
        + [jax.ShapeDtypeStruct((rows, width), jnp.bfloat16)],
        in_specs=[pl.BlockSpec(memory_space=pl.ANY)] * 4 + [whole] * 10,
        out_specs=[pl.BlockSpec(memory_space=pltpu.VMEM)] * 5,
        scratch_shapes=[pltpu.VMEM(shape, jnp.bfloat16) for shape in shapes]
        + [
            pltpu.VMEM((8, cols, 1, width), jnp.float32),
            pltpu.VMEM((rows, width), jnp.float32),
            pltpu.SemaphoreType.DMA((count,)),
            pltpu.SemaphoreType.DMA((4,)),
            pltpu.SemaphoreType.DMA((count,)),
            pltpu.SemaphoreType.DMA((count,)),
            pltpu.SemaphoreType.DMA((count,)),
            pltpu.SemaphoreType.DMA((4,)),
            pltpu.SemaphoreType.DMA((2,)),
            pltpu.SemaphoreType.DMA((2,)),
        ],
        compiler_params=pltpu.CompilerParams(
            collective_id=0, has_side_effects=True, vmem_limit_bytes=VMEM_LIMIT
        ),
    )(*weights, *lows, *highs, norm_train.reshape(1, width), norm_step.reshape(1, width))
    return (*results[:4], results[4].reshape(rows * width))


VMEM_LIMIT = 30 << 20


def local(
    rows,
    cols,
    w_query,
    low_query,
    high_query,
    w_key,
    low_key,
    high_key,
    w_value,
    low_value,
    high_value,
    w_mixed,
    low_mixed,
    high_mixed,
    norm_train,
    norm_step,
):
    weights = (w_query, w_key, w_value, w_mixed)
    lows = (low_query, low_key, low_value, low_mixed)
    highs = (high_query, high_key, high_value, high_mixed)
    if rows == SIDE * SIDE * 2 and cols > 1:
        return gather_kernel(cols, weights, lows, highs, norm_train, norm_step)
    pieces = [merged(*parts) for parts in zip(weights, lows, highs)]
    gathered = [
        lax.all_gather(piece, "rows", axis=axis, tiled=True)
        for piece, axis in zip(pieces, (0, 0, 0, 1))
    ]
    norm = lax.all_gather(
        (norm_train + norm_step).astype(jnp.bfloat16), ("rows", "cols"), axis=0, tiled=True
    )
    return (*gathered, norm)


def solution(mesh):
    in_specs = (
        P("rows", "cols"),
        P("rows", None),
        P(None, "cols"),
        P("rows", "cols"),
        P("rows", None),
        P(None, "cols"),
        P("rows", "cols"),
        P("rows", None),
        P(None, "cols"),
        P("cols", "rows"),
        P("cols", None),
        P(None, "rows"),
        P(("rows", "cols")),
        P(("rows", "cols")),
    )
    out_specs = (P(None, "cols"), P(None, "cols"), P(None, "cols"), P("cols", None), P())
    body = functools.partial(local, mesh.shape["rows"], mesh.shape["cols"])
    return jax.shard_map(body, mesh=mesh, in_specs=in_specs, out_specs=out_specs, check_vma=False)
```

time: 201 us -> 121 us (0.60)
  blocking collectives: 106 us -> 0 us
  Pallas kernels: 0 us -> 97.6 us
  waiting for transfers between devices: 53.4 us -> 0 us
  matrix products: 25.7 us -> 0 us
  local copies, waits for them, and re-layouts: 0.01 us -> 22 us
  between operations: 13.8 us -> 0.67 us
    all_gather x5 -> x0, blocking collectives: 106 us -> none  [the longest x1 70 us: local(): lax.all_gather((norm_train + norm_step).astype(jnp.bfloat16), ('rows', 'c...]
    pallas_call x0 -> x1, Pallas kernels: none -> 97.6 us  [gather_kernel(): pl.pallas_call(functools.partial(kernel, cols, chunks, split_dims), out_s...]
    all_gather x4 -> x0, waiting for transfers between devices: 50.8 us -> none  [the longest x1 46.1 us: local(): lax.all_gather(w_query, 'rows', axis=0, tiled=True)]
    dot_general x4 -> x0, matrix products: 25.7 us -> none  [the longest x1 9.15 us: local(): jnp.dot(low_mixed, factor_mixed, preferred_element_type=jnp.float32)]
    unnamed x4 -> x29, local copies, waits for them, and re-layouts: 0.01 us -> 22 us
    unnamed x4 -> x0, waiting for transfers between devices: 2.58 us -> none
  transfers between devices with their start and end apart: 4 -> 0, of which waited for: 2 -> 0; matrix products, arithmetic and copies ran while one was open for 9% -> 0% of each run, Pallas kernels for 0% -> 0%
where the time goes in v1:
time: 121 us; the launch traced here: 120 us
  Pallas kernels  97.6 us (81%)
  local copies, waits for them, and re-layouts  22 us (18%)
    pallas_call x1, Pallas kernels, gather_kernel(): pl.pallas_call(functools.partial(kernel, cols, chunks, split_dims), out_s...  97.6 us
    unnamed x29, local copies, waits for them, and re-layouts  22 us

profile of v1, /device:TPU:0, one launch (start us, length us, event | category | flops | bytes accessed | tf_op | source)
XLA Modules:
  0.0 120.3 jit_solution(6299492620931063777)
XLA Ops:
  0.6 0.8 copy.19.refs_4_
  1.5 0.8 copy.20.refs_5_
  2.3 0.8 copy.21.refs_6_
  3.2 0.9 copy.22.refs_7_
  4.1 0.0 copy-start
  4.1 1.2 %copy-done = bf16[512,1024]{1,0:T(8,128)(2,1)S(1)} copy-done((bf16[512,1024]{1,0:T(8,128)(2,1)S(1)}, bf16[512,1024]{1,0:T(8,128)(2,1)}, u32[]{:S(2)}) %copy-start) | copy-done | bytes 1048600
  5.3 0.0 copy-start.1
  5.3 1.2 %copy-done.1 = bf16[1024,512]{1,0:T(8,128)(2,1)S(1)} copy-done((bf16[1024,512]{1,0:T(8,128)(2,1)S(1)}, bf16[1024,512]{1,0:T(8,128)(2,1)}, u32[]{:S(2)}) %copy-start.1) | copy-done | bytes 1048600
  6.6 0.0 copy-start.2
  6.6 0.9 copy-done.2
  7.5 0.0 copy-start.3
  7.5 0.9 copy-done.3
  8.5 0.0 copy-start.4
  8.5 0.8 copy-done.4
  9.2 0.0 copy-start.5
  9.2 0.7 copy-done.5
  9.9 0.0 copy-start.6
  9.9 0.7 copy-done.6
  10.6 0.0 copy-start.7
  10.6 0.7 copy-done.7
  11.3 0.0 copy-start.8
  11.3 0.7 copy-done.8
  12.0 0.0 copy-start.9
  12.0 0.7 copy-done.9
  12.6 97.6 %shard_map.173 = (bf16[4096,1024]{1,0:T(8,128)(2,1)S(1)}, bf16[4096,256]{1,0:T(8,128)(2,1)S(1)}, bf16[4096,256]{1,0:T(8,128)(2,1)S(1)}, bf16[1024,4096]{1,0:T(8,128)(2,1)S(1)}, bf16[32,128]{1,0:T(8,128)(2,1)S(1)}) custom-call(bf16[512,1024]{1,0:T(8,128)(2,1)S(1)} %copy-done, bf16[512,256]{1,0:T(8,128)(2,1)S(1)} %copy-done.2, bf16[512,256]{1,0:T(8,128)(2,1)S(1)} %copy-done.3, ...), custom_call_target="tpu_custom_call" | custom-call | tf_op jit(solution)/shard_map/pallas_call | solution.py:183
  110.3 3.4 %copy.28 = bf16[4096,1024]{1,0:T(8,128)(2,1)} copy(bf16[4096,1024]{1,0:T(8,128)(2,1)S(1)} %get-tuple-element.15) | data formatting | bytes 16777216
  113.7 1.3 %copy.29 = bf16[4096,256]{1,0:T(8,128)(2,1)} copy(bf16[4096,256]{1,0:T(8,128)(2,1)S(1)} %get-tuple-element.16) | data formatting | bytes 4194304
  115.0 1.3 %copy.30 = bf16[4096,256]{1,0:T(8,128)(2,1)} copy(bf16[4096,256]{1,0:T(8,128)(2,1)S(1)} %get-tuple-element.17) | data formatting | bytes 4194304
  116.3 3.4 %copy.31 = bf16[1024,4096]{1,0:T(8,128)(2,1)} copy(bf16[1024,4096]{1,0:T(8,128)(2,1)S(1)} %get-tuple-element.18) | data formatting | bytes 16777216
  119.7 0.6 copy.32
Async XLA Ops:
  4.1 1.2 %copy-start = (bf16[512,1024]{1,0:T(8,128)(2,1)S(1)}, bf16[512,1024]{1,0:T(8,128)(2,1)}, u32[]{:S(2)}) copy-start(bf16[512,1024]{1,0:T(8,128)(2,1)} %refs_0_.1) | copy-start | bytes 3145732
  5.3 1.2 %copy-start.1 = (bf16[1024,512]{1,0:T(8,128)(2,1)S(1)}, bf16[1024,512]{1,0:T(8,128)(2,1)}, u32[]{:S(2)}) copy-start(bf16[1024,512]{1,0:T(8,128)(2,1)} %refs_3_.1) | copy-start | bytes 3145732
  6.6 0.9 copy-start.2
  7.5 0.9 copy-start.3
  8.5 0.8 copy-start.4
  9.2 0.7 copy-start.5
  9.9 0.7 copy-start.6
  10.6 0.7 copy-start.7
  11.3 0.7 copy-start.8
  12.0 0.7 copy-start.9

commit v2 on v1

--- a/solution.py
+++ b/solution.py
@@ -34,11 +34,11 @@
     *refs,
 ):
     weights, lows, highs = refs[0:4], refs[4:8], refs[8:12]
-    norm_train, norm_step = refs[12:14]
+    norms = refs[12:14]
     outs, norm_out = refs[14:18], refs[18]
-    held = refs[19:23]
-    norm_slots, norm_rows = refs[23:25]
-    load_sem, send_sem, x_sem, y_sem, far_sem, mate_sem, norm_send, norm_recv = refs[25:]
+    held, held_lows, held_highs, turned = refs[19:23], refs[23:27], refs[27:31], refs[31:35]
+    held_norms, norm_slots, norm_rows = refs[35:37], refs[37], refs[38]
+    load_sem, small_sem, send_sem, x_sem, y_sem, far_sem, mate_sem, norm_send, norm_recv = refs[39:]
 
     me, col = lax.axis_index("rows"), lax.axis_index("cols")
     core, x, y = me % 2, (me // 2) % 2, me // 4
@@ -89,8 +89,10 @@
             weights[index].at[piece, :], held[index].at[piece, :], load_sem.at[number]
         )
 
-    for number in range(len(chunks)):
-        load(number).start()
+    def small_load(number):
+        source = (*lows, *highs, *norms)[number]
+        target = (*held_lows, *held_highs, *held_norms)[number]
+        return pltpu.make_async_copy(source, target, small_sem.at[number])
 
     barrier = pltpu.get_barrier_semaphore()
     partners = [(lax.rem(me + step, 8), col) for step in range(1, 8)]
@@ -99,7 +101,16 @@
         pl.semaphore_signal(
             barrier, inc=1, device_id=partner, device_id_type=pl.DeviceIdType.MESH
         )
-    norm_slots[me, col] = norm_train[...] + norm_step[...]
+    begun = set()
+    for number in range(len(chunks)):
+        index = chunks[number][0]
+        if index not in begun:
+            begun.add(index)
+            small_load(index).start()
+            small_load(4 + index).start()
+        load(number).start()
+    small_load(8).start()
+    small_load(9).start()
     pl.semaphore_wait(barrier, len(partners) + len(mates))
 
     def send_own(number):
@@ -108,13 +119,19 @@
         send(me, number, across, y_sem.at[number])
         send(me, number, mate, mate_sem.at[index])
 
+    ready = set()
     for number, (index, first, rows) in enumerate(chunks):
+        if index not in ready:
+            ready.add(index)
+            small_load(index).wait()
+            small_load(4 + index).wait()
+            turned[index][...] = held_lows[index][...].astype(jnp.float32).T.astype(jnp.bfloat16)
         load(number).wait()
         piece = pl.ds(first, rows)
         place(me, chunks[number])[...] = merged(
             held[index][piece, :],
-            lows[index][piece, :],
-            highs[index][...],
+            turned[index][piece, :],
+            held_highs[index][...],
         )
         if number:
             send_own(number - 1)
@@ -129,6 +146,9 @@
             device_id_type=pl.DeviceIdType.MESH,
         )
 
+    small_load(8).wait()
+    small_load(9).wait()
+    norm_slots[me, col] = held_norms[0][...] + held_norms[1][...]
     for partner in mates:
         norm_copy(norm_slots.at[me, col], partner, 0).start()
     send_own(len(chunks) - 1)
@@ -171,6 +191,7 @@
 
 def gather_kernel(cols, weights, lows, highs, norm_train, norm_step):
     split_dims = (0, 0, 0, 1)
+    lows = [low.T for low in lows]
     shapes = [weight.shape for weight in weights]
     chunks = plan_chunks(shapes)
     full = [
@@ -180,17 +201,23 @@
     rows, width = 8 * cols, norm_train.shape[0]
     whole = pl.BlockSpec(memory_space=pltpu.VMEM)
     count = len(chunks)
+    kept = 2 * (sum(height * across for height, across in full) + rows * width)
     results = pl.pallas_call(
         functools.partial(kernel, cols, chunks, split_dims),
         out_shape=[pltpu.VMEM(shape, jnp.bfloat16) for shape in full]
-        + [jax.ShapeDtypeStruct((rows, width), jnp.bfloat16)],
-        in_specs=[pl.BlockSpec(memory_space=pl.ANY)] * 4 + [whole] * 10,
-        out_specs=[pl.BlockSpec(memory_space=pltpu.VMEM)] * 5,
+        + [pltpu.VMEM((rows, width), jnp.bfloat16)],
+        in_specs=[pl.BlockSpec(memory_space=pltpu.HBM)] * 14,
+        out_specs=[whole] * 5,
         scratch_shapes=[pltpu.VMEM(shape, jnp.bfloat16) for shape in shapes]
+        + [pltpu.VMEM(low.shape, jnp.bfloat16) for low in lows]
+        + [pltpu.VMEM(high.shape, jnp.bfloat16) for high in highs]
+        + [pltpu.VMEM(low.shape[::-1], jnp.bfloat16) for low in lows]
+        + [pltpu.VMEM((1, width), jnp.float32)] * 2
         + [
             pltpu.VMEM((8, cols, 1, width), jnp.float32),
             pltpu.VMEM((rows, width), jnp.float32),
             pltpu.SemaphoreType.DMA((count,)),
+            pltpu.SemaphoreType.DMA((10,)),
             pltpu.SemaphoreType.DMA((4,)),
             pltpu.SemaphoreType.DMA((count,)),
             pltpu.SemaphoreType.DMA((count,)),
@@ -200,13 +227,50 @@
             pltpu.SemaphoreType.DMA((2,)),
         ],
         compiler_params=pltpu.CompilerParams(
-            collective_id=0, has_side_effects=True, vmem_limit_bytes=VMEM_LIMIT
+            collective_id=0, has_side_effects=True, vmem_limit_bytes=VMEM_BYTES - kept
         ),
     )(*weights, *lows, *highs, norm_train.reshape(1, width), norm_step.reshape(1, width))
+    results = write_out(results)
     return (*results[:4], results[4].reshape(rows * width))
 
 
-VMEM_LIMIT = 30 << 20
+VMEM_BYTES = 67043328
+WRITE_PIECES = 4
+
+
+def write_kernel(*refs):
+    count = len(refs) // 2
+    sources, targets, sem = refs[:count], refs[count:-1], refs[-1]
+    copies = []
+    for index in range(count):
+        height = sources[index].shape[0]
+        pieces = WRITE_PIECES if height >= 1024 else 1
+        for piece in range(pieces):
+            part = pl.ds(piece * (height // pieces), height // pieces)
+            copies.append(
+                pltpu.make_async_copy(
+                    sources[index].at[part, :],
+                    targets[index].at[part, :],
+                    sem.at[index * WRITE_PIECES + piece],
+                )
+            )
+            copies[-1].start()
+    for copy in copies:
+        copy.wait()
+
+
+def write_out(arrays):
+    return pl.pallas_call(
+        write_kernel,
+        out_shape=[jax.ShapeDtypeStruct(array.shape, array.dtype) for array in arrays],
+        in_specs=[pl.BlockSpec(memory_space=pltpu.VMEM)] * len(arrays),
+        out_specs=[pl.BlockSpec(memory_space=pltpu.HBM)] * len(arrays),
+        scratch_shapes=[pltpu.SemaphoreType.DMA((len(arrays) * WRITE_PIECES,))],
+        compiler_params=pltpu.CompilerParams(vmem_limit_bytes=WRITE_LIMIT),
+    )(*arrays)
+
+
+WRITE_LIMIT = 1 << 20
 
 
 def local(

time: 121 us -> 102 us (0.84)
  local copies, waits for them, and re-layouts: 22 us -> 0 us
  Pallas kernels: 97.6 us -> 101 us
    unnamed x29 -> x0, local copies, waits for them, and re-layouts: 22 us -> none
    pallas_call x0 -> x1, Pallas kernels: none -> 7.29 us  [write_out(): pl.pallas_call(write_kernel, out_shape=[jax.ShapeDtypeStruct(array.shape,...]
    pallas_call x1, Pallas kernels: 97.6 us -> 94.1 us  [gather_kernel(): pl.pallas_call(functools.partial(kernel, cols, chunks, split_dims), out_s...]
where the time goes in v2:
time: 102 us
  Pallas kernels  101 us (99%)
    pallas_call x1, Pallas kernels, gather_kernel(): pl.pallas_call(functools.partial(kernel, cols, chunks, split_dims), out_s...  94.1 us
    pallas_call x1, Pallas kernels, write_out(): pl.pallas_call(write_kernel, out_shape=[jax.ShapeDtypeStruct(array.shape,...  7.29 us

profile of v2, /device:TPU:0, one launch (start us, length us, event | category | flops | bytes accessed | tf_op | source)
XLA Modules:
  0.0 102.0 jit_solution(13254493475894853397)
XLA Ops:
  0.6 94.1 %shard_map.173 = (bf16[4096,1024]{1,0:T(8,128)(2,1)S(1)}, bf16[4096,256]{1,0:T(8,128)(2,1)S(1)}, bf16[4096,256]{1,0:T(8,128)(2,1)S(1)}, bf16[1024,4096]{1,0:T(8,128)(2,1)S(1)}, bf16[32,128]{1,0:T(8,128)(2,1)S(1)}) custom-call(bf16[512,1024]{1,0:T(8,128)(2,1)} %refs_0_.1, bf16[512,256]{1,0:T(8,128)(2,1)} %refs_1_.1, bf16[512,256]{1,0:T(8,128)(2,1)} %refs_2_.1, ...), custom_call_target="tpu_custom_call" | custom-call | tf_op jit(solution)/shard_map/pallas_call | solution.py:205
  94.8 7.3 %shard_map.174 = (bf16[4096,1024]{1,0:T(8,128)(2,1)}, bf16[4096,256]{1,0:T(8,128)(2,1)}, bf16[4096,256]{1,0:T(8,128)(2,1)}, bf16[1024,4096]{1,0:T(8,128)(2,1)}, bf16[32,128]{1,0:T(8,128)(2,1)}) custom-call(bf16[4096,1024]{1,0:T(8,128)(2,1)S(1)} %get-tuple-element.15.refs_0_, bf16[4096,256]{1,0:T(8,128)(2,1)S(1)} %get-tuple-element.16.refs_1_, ...), custom_call_target="tpu_custom_call" | custom-call | tf_op jit(solution)/shard_map/pallas_call | solution.py:263
